TPU v7x, 32 devices: a whole 2x2x4 slice. The times are simulated.
32 devices in a mesh: member: 2 (over x), row: 16 (over z, y, core).
Axes of the slice: x: 2, y: 2, z: 4, core: 2. Of those that a mesh axis runs over, the one named last changes fastest.
Arguments:
- field: float32 [8, 6, 2048, 2048], P('member', None, 'row'), parts along dimension 0, as said below
- host: float32 [128, 2, 8, 6, 128], P('row', None, 'member'), parts along dimension 2, may hold values from -0.12 to 0.12
- weights: float32 [8, 4], replicated, may hold values from 0.1 to 1
- cut_x: int32 [6], replicated, may hold values from 16 to 63
- cut_y: int32 [6], replicated, may hold values from 16 to 63
- table_index: int32 [6], replicated, may hold values from 0 to 7
Outputs:
- nudged: float32 [8, 6, 2048, 2048], P('member', None, 'row'), parts along dimension 0
There are 2 independent parts, one for each index of `member`. A program takes and returns all parts, laid end to end along the dimension named above; an argument that names none is the same for every part. Nothing has to cross between parts.
Inputs may be any that keep to these rules, and one draw needn't show every extreme that they name: `field`: real-valued fields with strong large-scale structure.
All inputs are finite; a program needn't handle non-finite values.
Results may differ from a plain program's by a relative error of at most 0.00005.
Values sent between devices are 32-bit elements; how exact they have to be, the bound alone decides.
A program may use at most 128 MiB of HBM per device.

v0:
```python
import functools
import math

import jax
import jax.numpy as jnp
import numpy as np
from jax import lax
from jax.experimental import pallas as pl
from jax.experimental.pallas import tpu as pltpu
from jax.sharding import PartitionSpec as P

TABLE = 8
MESH = pl.DeviceIdType.MESH
VMEM_BYTES = 63_000_000
HIGHEST = lax.Precision.HIGHEST


def box_wave(index, khalf):
    half = index // 2
    return jnp.where(index % 2 == 0, half, jnp.where(index == 1, -khalf, -half))


def wave_tables(positions, length, waves):
    phase = jnp.mod(positions[:, None] * waves[None, :], length).astype(jnp.float32) * (
        2.0 * math.pi / length
    )
    return (jnp.cos(phase), jnp.sin(phase))


def general(field, host, weights, cut_x, cut_y, table_index):
    variables, levels, row_count, ny = field.shape
    owned, kbox = host.shape[0], host.shape[-1]
    fields = variables * levels
    devices = lax.axis_size("row")
    nx = row_count * devices
    place = lax.axis_index("row")
    local_rows = place * row_count + lax.iota(jnp.int32, row_count)
    x_waves = lax.iota(jnp.int32, kbox) - kbox // 2
    y_waves = box_wave(lax.iota(jnp.int32, kbox), kbox // 2)
    own_waves = box_wave(place * owned + lax.iota(jnp.int32, owned), kbox // 2)
    onehot = (table_index[:, None] == lax.iota(jnp.int32, TABLE)[None, :]).astype(jnp.float32)
    blend = jnp.dot(onehot, weights, precision=HIGHEST)
    mask_x = (jnp.abs(x_waves)[None, :] <= cut_x[:, None]).astype(jnp.float32)
    mask_y = (jnp.abs(own_waves)[None, :] <= cut_y[:, None]).astype(jnp.float32)
    scale = blend.T[:, :, None, None] * mask_y[None, :, :, None] * mask_x[None, :, None, :]
    cos_y, sin_y = wave_tables(lax.iota(jnp.int32, ny), ny, y_waves)
    cos_x, sin_x = wave_tables(local_rows, nx, x_waves)
    table_y = jnp.concatenate([cos_y, -sin_y], 1)
    table_x = jnp.stack([jnp.concatenate([cos_x, -sin_x], 1), jnp.concatenate([sin_x, cos_x], 1)])

    def one(pair):
        grid, wanted, factor = pair
        spread = jnp.dot(grid, table_y, precision=HIGHEST).reshape(row_count, 2, kbox)
        parts = jnp.einsum("xck,cxq->kq", spread, table_x, precision=HIGHEST)
        parts = parts.reshape(devices, owned, 2, kbox)
        moved = lax.all_to_all(parts, "row", split_axis=0, concat_axis=0, tiled=True)
        spectrum = jnp.sum(moved, 0) / (nx * ny)
        delta = factor[:, None, :] * (wanted - spectrum)
        box = lax.all_gather(delta, "row", axis=0, tiled=True).reshape(kbox, 2 * kbox)
        back = jnp.einsum("kq,cxq->xck", box, table_x, precision=HIGHEST)
        return grid + jnp.dot(back.reshape(row_count, 2 * kbox), table_y.T, precision=HIGHEST)

    wanted = host.transpose(2, 3, 0, 1, 4).reshape(fields, owned, 2, kbox)
    result = lax.map(
        one, (field.reshape(fields, row_count, ny), wanted, scale.reshape(fields, owned, kbox))
    )
    return result.reshape(field.shape)


def halves(values):
    high = values.astype(jnp.bfloat16)
    return high, (values - high.astype(jnp.float32)).astype(jnp.bfloat16)


def np_halves(values):
    values = values.astype(np.float32)
    high = values.astype(jnp.bfloat16)
    return high, (values - high.astype(np.float32)).astype(jnp.bfloat16)


def real_modes(positions, length, waves, is_sine):
    if isinstance(positions, int):
        positions = np.arange(positions)
    phase = (positions[:, None] * waves[None, :]) % length * (2.0 * np.pi / length)
    return np.where(is_sine[None, :], np.sin(phase), np.cos(phase))


def local_modes(base_ref, turn_ref):
    count = base_ref.shape[0] // 2
    return base_ref[:count] * turn_ref[0, :1] + base_ref[count:] * turn_ref[0, 1:2]


def inverse_kernel(field_ref, modes_ref, table_ref, base_ref, turn_ref, out_ref, three_ref):
    _, count, row_count, ny = field_ref.shape
    kbox = base_ref.shape[1]
    owned = modes_ref.shape[2] // count
    x_high, x_low = halves(local_modes(base_ref, turn_ref))
    x_three = jnp.concatenate([x_high, x_high, x_low], 1)

    @pl.when((pl.program_id(0) == 0) & (pl.program_id(1) == 0))
    def _():
        three_ref[:kbox] = table_ref[:kbox]
        three_ref[kbox:] = table_ref[...]

    parts = []
    for k in range(count):
        high, low = halves(modes_ref[0, :, k * owned : (k + 1) * owned].reshape(kbox, kbox))
        parts.append(
            lax.dot_general(
                x_three,
                jnp.concatenate([high, low, high], 1),
                (((1,), (1,)), ((), ())),
                preferred_element_type=jnp.float32,
            )
        )
    high, low = halves(jnp.concatenate(parts, 0))
    added = jnp.dot(
        jnp.concatenate([high, low, high], 1), three_ref[...], preferred_element_type=jnp.float32
    )
    out_ref[...] = field_ref[...] + added.reshape(field_ref.shape)


def stage_step(stage):
    return 2 * stage + 1


def box_kernel(
    bits, chunks, norm, weights_ref, cut_x_ref, cut_y_ref, index_ref, field_ref, table_ref, base_ref,
    turn_ref, host_ref, mix_ref, out_ref, edge_ref, part_ref, full_ref, *scratch
):
    got, kept = scratch[:bits], scratch[bits : 2 * bits]
    send_sem, recv_sem, out_sem = scratch[2 * bits :]
    _, group, row_count, ny = field_ref.shape
    span, kbox = host_ref.shape[-2:]
    owned, khalf, levels = span // group, kbox // 2, cut_x_ref.shape[0]
    half = owned // 2
    now = pl.program_id(0)
    me = lax.axis_index("row")
    member = lax.axis_index("member")
    mine = [(me // (1 << b)) % 2 for b in range(bits)]
    peer = [me + (1 << b) * (1 - 2 * mine[b]) for b in range(bits)]
    barrier = pltpu.get_barrier_semaphore()

    @pl.when(now == 0)
    def _():
        for b in range(bits):
            pl.semaphore_signal(barrier, inc=1, device_id=(member, peer[b]), device_id_type=MESH)
        edge = cut_x_ref[0]
        for level in range(levels):
            edge = jnp.maximum(edge, jnp.maximum(cut_x_ref[level], cut_y_ref[level]))
        edge_ref[0] = edge

    def lead(step, bit_value):
        return (slice(None),) * (bits - 1 - step) + (bit_value,)

    def remote(source, target, stage, chunk, bit):
        return pltpu.make_async_remote_copy(
            src_ref=source,
            dst_ref=target,
            send_sem=send_sem.at[chunk, stage],
            recv_sem=recv_sem.at[chunk, stage],
            device_id=(member, peer[bit]),
            device_id_type=MESH,
        )

    def held(step):
        return part_ref if step == 0 else kept[step - 1]

    def reduce_copy(step, chunk):
        source = held(step).at[(chunk,) + lead(step, 1 - mine[step])]
        return remote(source, got[step].at[chunk], step, chunk, step)

    def gather_copy(step, chunk):
        fixed = tuple(mine[b] for b in range(step, -1, -1))
        block = full_ref.at[(chunk,) + (slice(None),) * (bits - 1 - step) + fixed]
        return remote(block, block, bits + step, chunk, step)

    def out_copy(chunk):
        return pltpu.make_async_copy(full_ref.at[chunk], out_ref.at[chunk], out_sem.at[chunk])

    slot = lax.broadcasted_iota(jnp.int32, (span, kbox), 0)
    column = lax.broadcasted_iota(jnp.int32, (span, kbox), 1)
    line = slot % owned < half

    def swap(values):
        return jnp.where(
            line, pltpu.roll(values, span - half, 0), pltpu.roll(values, half, 0)
        )

    def mixed(values, axis):
        total = 0.0
        for _ in range(3):
            piece = values.astype(jnp.bfloat16)
            values = values - piece.astype(jnp.float32)
            total = total + lax.dot_general(
                piece,
                mix_ref[...],
                (((1,), (axis,)), ((), ())),
                preferred_element_type=jnp.float32,
            )
        return total

    def pull(chunk):
        both = mixed(kept[bits - 1][chunk] * norm, 0)
        even, odd = both[:, :kbox], both[:, kbox:]
        even_s, odd_s = swap(even), swap(odd)
        real = jnp.where(line, even - odd_s, even_s + odd)
        imag = jnp.where(line, -(odd + even_s), even - odd_s)
        wave = me * half + slot % half
        wave = jnp.where((wave == 0) & (slot % owned >= half), khalf, wave)
        steps = levels // group
        scale = jnp.zeros((span, kbox), jnp.float32)
        for k in range(group):
            level = (chunk % steps) * group + k
            inside = (jnp.abs(column - khalf) <= cut_x_ref[level]) & (wave <= cut_y_ref[level])
            blend = jnp.where(inside, weights_ref[chunk // steps, index_ref[level]], 0.0)
            scale = jnp.where(slot // owned == k, blend, scale)
        real = scale * (host_ref[0, chunk] - real)
        imag = scale * (host_ref[1, chunk] - imag)
        real_s, imag_s = swap(real), swap(imag)
        cosine = jnp.where(line, real + real_s, imag - imag_s)
        sine = jnp.where(line, -(imag + imag_s), real - real_s)
        own = tuple(mine[b] for b in range(bits - 1, -1, -1))
        full_ref[(chunk,) + own] = mixed(jnp.concatenate([cosine, sine], 1), 1)

    def advance(stage, chunk):
        if stage < bits:
            reduce_copy(stage, chunk).wait()
            own = held(stage)[(chunk,) + lead(stage, mine[stage])]
            kept[stage][chunk] = own + got[stage][chunk]
            if stage + 1 < bits:
                reduce_copy(stage + 1, chunk).start()
            else:
                pull(chunk)
                gather_copy(bits - 1, chunk).start()
        else:
            step = 2 * bits - 1 - stage
            gather_copy(step, chunk).wait()
            if step > 0:
                gather_copy(step - 1, chunk).start()
            else:
                out_copy(chunk).start()

    @pl.when(now < chunks)
    def _():
        high, low = halves(field_ref[...].reshape(group * row_count, ny))
        both = jnp.dot(high, table_ref[...], preferred_element_type=jnp.float32)
        rest = jnp.dot(low, table_ref[:, :kbox], preferred_element_type=jnp.float32)
        part = both[:, :kbox] + both[:, kbox:] + rest
        x_high, x_low = halves(local_modes(base_ref, turn_ref))
        x_three = jnp.concatenate([x_high, x_high, x_low], 0)
        cube = (2,) * bits
        for k in range(group):
            high, low = halves(part[k * row_count : (k + 1) * row_count])
            moded = lax.dot_general(
                jnp.concatenate([high, low, high], 0),
                x_three,
                (((0,), (0,)), ((), ())),
                preferred_element_type=jnp.float32,
            )
            where = (now,) + (slice(None),) * bits + (slice(k * owned, (k + 1) * owned),)
            part_ref[where] = moded.reshape(cube + (owned, kbox))

    @pl.when(now == 0)
    def _():
        pl.semaphore_wait(barrier, bits)

    for stage in range(2 * bits):
        chunk = now - stage_step(stage)

        @pl.when((chunk >= 0) & (chunk < chunks))
        def _(stage=stage, chunk=chunk):
            advance(stage, chunk)

    @pl.when(now < chunks)
    def _():
        reduce_copy(0, now).start()

    @pl.when(now == pl.num_programs(0) - 1)
    def _():
        for chunk in range(chunks):
            out_copy(chunk).wait()


def box_modes(scalars, field, table, base, turn, host, mix, group):
    variables, levels, row_count, ny = field.shape
    devices, kbox = turn.shape[0], host.shape[-1]
    chunks, span = host.shape[1:3]
    steps = levels // group
    bits = devices.bit_length() - 1
    cube = (2,) * bits
    sizes = [
        pltpu.VMEM((chunks,) + (2,) * (bits - 1 - step) + (span, kbox), jnp.float32)
        for step in range(bits)
    ]

    def chunk_at(now):
        chunk = jnp.minimum(now, chunks - 1)
        return (chunk // steps, chunk % steps, 0, 0)

    def whole(array):
        return pl.BlockSpec(array.shape, lambda now: (0,) * array.ndim)

    smem = pl.BlockSpec(memory_space=pltpu.SMEM)
    return pl.pallas_call(
        functools.partial(box_kernel, bits, chunks, 1.0 / (row_count * devices * ny)),
        grid=(chunks + stage_step(2 * bits - 1),),
        out_shape=(
            jax.ShapeDtypeStruct((chunks,) + cube + (span, kbox), jnp.float32),
            jax.ShapeDtypeStruct((1,), jnp.int32),
        ),
        in_specs=[smem] * 4
        + [
            pl.BlockSpec((1, group, row_count, ny), chunk_at),
            whole(table),
            whole(base),
            pl.BlockSpec((1, 2, kbox), lambda now: (lax.axis_index("row"), 0, 0)),
            whole(host),
            whole(mix),
        ],
        out_specs=(pl.BlockSpec(memory_space=pl.ANY), smem),
        scratch_shapes=[pltpu.VMEM((chunks,) + cube + (span, kbox), jnp.float32)] * 2
        + sizes * 2
        + [
            pltpu.SemaphoreType.DMA((chunks, 2 * bits)),
            pltpu.SemaphoreType.DMA((chunks, 2 * bits)),
            pltpu.SemaphoreType.DMA((chunks,)),
        ],
        compiler_params=pltpu.CompilerParams(
            collective_id=0, has_side_effects=True, vmem_limit_bytes=VMEM_BYTES
        ),
    )(*scalars, field, table, base, turn, host, mix)


def nudge(field, host, weights, cut_x, cut_y, table_index):
    variables, levels, row_count, ny = field.shape
    owned, kbox = host.shape[0], host.shape[-1]
    khalf, half = kbox // 2, owned // 2
    devices = lax.axis_size("row")
    nx = row_count * devices
    fields = variables * levels

    column = np.arange(kbox)
    y_wave = column // owned * half + column % half
    y_sine = column % owned >= half
    y_high, y_low = np_halves(real_modes(ny, ny, y_wave, y_sine))
    table_y = jnp.asarray(np.concatenate([y_high, y_low], 1))
    table_back = jnp.asarray(np.concatenate([y_high.T, y_low.T], 0))
    x_wave, x_sine = column % khalf, column >= khalf
    start = np.arange(devices) * row_count
    base = np.concatenate(
        [real_modes(row_count, nx, x_wave, column < 0), real_modes(row_count, nx, x_wave, column >= 0)]
    )
    turn_cos = real_modes(start, nx, x_wave, column < 0)
    turn_sin = real_modes(start, nx, x_wave, column >= 0)
    turn = np.stack(
        [np.where(x_sine, turn_sin, turn_cos), np.where(x_sine, turn_cos, -turn_sin)], 1
    )
    base = jnp.asarray(base.astype(np.float32))
    turn = jnp.asarray(turn.astype(np.float32))
    wave = column - khalf
    inside = np.abs(wave) < khalf
    mc = ((column[:, None] == np.abs(wave)[None, :]) & inside).astype(np.float32)
    ms = ((column[:, None] == np.abs(wave)[None, :] + khalf) & inside) * np.sign(wave)
    ms = ms.astype(np.float32)

    group = levels
    steps = levels // group
    grid_block = pl.BlockSpec((1, group, row_count, ny), lambda v, g: (v, g, 0, 0))
    span = group * owned
    mode_block = pl.BlockSpec(
        (1, devices, span, kbox), lambda v, g: (v * steps + g, 0, 0, 0)
    )

    def whole(*shape):
        return pl.BlockSpec(shape, lambda v, g: (0,) * len(shape))

    local_turn = pl.BlockSpec((1, 2, kbox), lambda v, g: (lax.axis_index("row"), 0, 0))
    params = pltpu.CompilerParams(vmem_limit_bytes=VMEM_BYTES)
    placed = host.reshape(half, 2, 2, fields, kbox).transpose(2, 3, 1, 0, 4)
    modes, edge = box_modes(
        (weights.T, cut_x, cut_y, table_index),
        field,
        table_y,
        base,
        turn,
        placed.reshape(2, fields // group, span, kbox),
        jnp.asarray(np.concatenate([mc, ms], 1)).astype(jnp.bfloat16),
        group,
    )
    modes = modes.reshape(fields // group, devices, span, kbox)

    inverse = pl.pallas_call(
        inverse_kernel,
        grid=(variables, steps),
        out_shape=jax.ShapeDtypeStruct(field.shape, jnp.float32),
        in_specs=[grid_block, mode_block, whole(2 * kbox, ny), whole(2 * row_count, kbox), local_turn],
        out_specs=grid_block,
        scratch_shapes=[pltpu.VMEM((3 * kbox, ny), jnp.bfloat16)],
        compiler_params=params,
    )
    return lax.cond(
        edge[0] >= khalf,
        lambda *args: general(*args[:6]),
        lambda *args: inverse(args[0], *args[6:]),
        field, host, weights, cut_x, cut_y, table_index, modes, table_back, base, turn,
    )


def solution(mesh):
    return jax.shard_map(
        nudge,
        mesh=mesh,
        in_specs=(
            P("member", None, "row", None),
            P("row", None, "member", None, None),
            P(),
            P(),
            P(),
            P(),
        ),
        out_specs=P("member", None, "row", None),
        check_vma=False,
    )
```

profile of v0, /device:TPU:0, one launch (start us, length us, event | category | flops | bytes accessed | tf_op | source)
XLA Modules:
  0.0 65.1 jit_solution(16496786453910984344)
XLA Ops:
  0.0 0.0 copy-start.1
  0.0 0.0 copy-start.2
  0.0 0.0 copy-start
  0.0 0.0 copy-start.3
  0.0 0.0 copy-start.4
  0.0 0.0 copy-start.5
  0.0 0.0 copy-start.6
  0.0 1.1 %copy.23 = f32[8,2,4,6,128]{4,0,3,2,1:T(8,128)S(1)} copy(f32[8,2,4,6,128]{4,2,3,1,0:T(4,128)} %param.16) | data formatting | bytes 393216 | tf_op args[1]
  1.1 0.7 %copy.24 = f32[2,24,2,4,128]{4,3,2,1,0:T(4,128)} copy(f32[2,24,2,4,128]{4,2,3,1,0:T(2,128)S(1)} %bitcast.89) | data formatting | bytes 393216 | tf_op jit(solution)/shard_map/transpose | solution.py:380
  1.8 43.3 %shard_map.112 = (f32[4,2,2,2,2,48,128]{6,5,4,3,2,1,0:T(8,128)S(1)}, s32[1]{0:T(128)}) custom-call(f32[4,8]{1,0:T(4,128)} %bitcast.91, s32[6]{0:T(128)} %cut_x_ref.1, s32[6]{0:T(128)} %cut_y_ref.1, s32[6]{0:T(128)} %index_ref.1, f32[4,6,128,2048]{3,2,1,0:T(8,128)} %field_ref.1, bf16[2048,256]{1,0:T(8,128)(2,1)} %constant.121.clone.table_ref, ...), custom_call_target="tpu_custom_call" | custom-call | tf_op jit(solution)/shard_map/pallas_call | solution.py:305
  45.8 0.0 copy-done.1
  45.8 0.0 copy-done.2
  45.8 0.0 copy-done
  45.8 0.0 copy-done.3
  45.8 0.0 copy-done.4
  45.8 0.0 copy-done.5
  45.8 0.0 copy-done.6
  45.9 19.2 %conditional.1 = (f32[4,6,128,2048]{3,2,1,0:T(8,128)}) conditional(s32[]{:T(128)} %bitcast.23, (f32[4,6,128,2048]{3,2,1,0:T(8,128)}, f32[4,2,2,2,2,48,128]{6,5,4,3,2,1,0:T(8,128)S(1)}, (), f32[256,128]{1,0:T(8,128)S(1)}, f32[16,2,128]{2,1,0:T(2,128)S(1)}) %tuple.45, (f32[4,6,128,2048]{3,2,1,0:T(8,128)}, f32[8,2,4,6,128]{4,2,3,1,0:T(4,128)S(1)}, ...), branch_computations={%region_0.0_spmd, %region_1.5_spmd} | conditional | flops 1817103232 | bytes 17667372 | solution.py:402
  45.9 19.2 %branch_0_fun.1 = f32[4,6,128,2048]{3,2,1,0:T(8,128)} custom-call(f32[4,6,128,2048]{3,2,1,0:T(8,128)} %get-tuple-element.58.field_ref, f32[4,16,48,128]{3,2,1,0:T(8,128)S(1)} %bitcast.87, bf16[256,2048]{1,0:T(8,128)(2,1)} %constant.122.clone.1.table_ref, f32[256,128]{1,0:T(8,128)S(1)} %get-tuple-element.61.base_ref, f32[16,2,128]{2,1,0:T(2,128)S(1)} %get-tuple-element.62.turn_ref), custom_call_target="tpu_custom_call" | custom-call | tf_op jit(solution)/shard_map/cond/branch_0_fun/pallas_call | solution.py:405
Async XLA Ops:
  0.0 45.8 %copy-start.1 = (f32[256,128]{1,0:T(8,128)S(1)}, f32[256,128]{1,0:T(8,128)}, u32[]{:S(2)}) copy-start(f32[256,128]{1,0:T(8,128)} %constant.123.clone.base_ref) | copy-start | bytes 393220
  0.0 45.8 %copy-start.2 = (f32[16,2,128]{2,1,0:T(2,128)S(1)}, f32[16,2,128]{2,1,0:T(2,128)}, u32[]{:S(2)}) copy-start(f32[16,2,128]{2,1,0:T(2,128)} %constant.124.clone.turn_ref) | copy-start | bytes 49156
  0.0 45.8 %copy-start = (f32[8,2,4,6,128]{4,2,3,1,0:T(4,128)S(1)}, f32[8,2,4,6,128]{4,2,3,1,0:T(4,128)}, u32[]{:S(2)}) copy-start(f32[8,2,4,6,128]{4,2,3,1,0:T(4,128)} %param.16) | copy-start | bytes 589828
  0.0 45.8 %copy-start.3 = (f32[8,4]{0,1:T(4,128)S(1)}, f32[8,4]{0,1:T(4,128)}, u32[]{:S(2)}) copy-start(f32[8,4]{0,1:T(4,128)} %param.17) | copy-start | bytes 388
  0.0 45.8 %copy-start.4 = (s32[6]{0:T(128)S(1)}, s32[6]{0:T(128)}, u32[]{:S(2)}) copy-start(s32[6]{0:T(128)} %cut_x_ref.1) | copy-start | bytes 76
  0.0 45.8 %copy-start.5 = (s32[6]{0:T(128)S(1)}, s32[6]{0:T(128)}, u32[]{:S(2)}) copy-start(s32[6]{0:T(128)} %cut_y_ref.1) | copy-start | bytes 76
  0.0 45.8 %copy-start.6 = (s32[6]{0:T(128)S(1)}, s32[6]{0:T(128)}, u32[]{:S(2)}) copy-start(s32[6]{0:T(128)} %index_ref.1) | copy-start | bytes 76
where the time goes:
time: 65.3 us; the launch traced here: 65.1 us
  Pallas kernels  62.5 us (96%)
  local copies, waits for them, and re-layouts  1.82 us (3%)
  between operations  0.71 us (1%)
    pallas_call x1, Pallas kernels, box_modes(): pl.pallas_call(functools.partial(box_kernel, bits, chunks, 1.0 / (row_cou...  43.3 us
    pallas_call x1, Pallas kernels, nudge(): inverse(args[0], *args[6:])  19.2 us

commit v1 on v0

v1 whole, which is shorter than its diff:
```python
import functools
import math

import jax
import jax.numpy as jnp
import numpy as np
from jax import lax
from jax.experimental import pallas as pl
from jax.experimental.pallas import tpu as pltpu
from jax.sharding import PartitionSpec as P

TABLE = 8
MESH = pl.DeviceIdType.MESH
VMEM_BYTES = 36_000_000
GROUP = 3
LAGS = (1, 2, 3)
PREPARE = 1
HIGHEST = lax.Precision.HIGHEST


def box_wave(index, khalf):
    half = index // 2
    return jnp.where(index % 2 == 0, half, jnp.where(index == 1, -khalf, -half))


def wave_tables(positions, length, waves):
    phase = jnp.mod(positions[:, None] * waves[None, :], length).astype(jnp.float32) * (
        2.0 * math.pi / length
    )
    return (jnp.cos(phase), jnp.sin(phase))


def general(field, host, weights, cut_x, cut_y, table_index):
    variables, levels, row_count, ny = field.shape
    owned, kbox = host.shape[0], host.shape[-1]
    fields = variables * levels
    devices = lax.axis_size("row")
    nx = row_count * devices
    place = lax.axis_index("row")
    local_rows = place * row_count + lax.iota(jnp.int32, row_count)
    x_waves = lax.iota(jnp.int32, kbox) - kbox // 2
    y_waves = box_wave(lax.iota(jnp.int32, kbox), kbox // 2)
    own_waves = box_wave(place * owned + lax.iota(jnp.int32, owned), kbox // 2)
    onehot = (table_index[:, None] == lax.iota(jnp.int32, TABLE)[None, :]).astype(jnp.float32)
    blend = jnp.dot(onehot, weights, precision=HIGHEST)
    mask_x = (jnp.abs(x_waves)[None, :] <= cut_x[:, None]).astype(jnp.float32)
    mask_y = (jnp.abs(own_waves)[None, :] <= cut_y[:, None]).astype(jnp.float32)
    scale = blend.T[:, :, None, None] * mask_y[None, :, :, None] * mask_x[None, :, None, :]
    cos_y, sin_y = wave_tables(lax.iota(jnp.int32, ny), ny, y_waves)
    cos_x, sin_x = wave_tables(local_rows, nx, x_waves)
    table_y = jnp.concatenate([cos_y, -sin_y], 1)
    table_x = jnp.stack([jnp.concatenate([cos_x, -sin_x], 1), jnp.concatenate([sin_x, cos_x], 1)])

    def one(pair):
        grid, wanted, factor = pair
        spread = jnp.dot(grid, table_y, precision=HIGHEST).reshape(row_count, 2, kbox)
        parts = jnp.einsum("xck,cxq->kq", spread, table_x, precision=HIGHEST)
        parts = parts.reshape(devices, owned, 2, kbox)
        moved = lax.all_to_all(parts, "row", split_axis=0, concat_axis=0, tiled=True)
        spectrum = jnp.sum(moved, 0) / (nx * ny)
        delta = factor[:, None, :] * (wanted - spectrum)
        box = lax.all_gather(delta, "row", axis=0, tiled=True).reshape(kbox, 2 * kbox)
        back = jnp.einsum("kq,cxq->xck", box, table_x, precision=HIGHEST)
        return grid + jnp.dot(back.reshape(row_count, 2 * kbox), table_y.T, precision=HIGHEST)

    wanted = host.transpose(2, 3, 0, 1, 4).reshape(fields, owned, 2, kbox)
    result = lax.map(
        one, (field.reshape(fields, row_count, ny), wanted, scale.reshape(fields, owned, kbox))
    )
    return result.reshape(field.shape)


def halves(values):
    high = values.astype(jnp.bfloat16)
    return high, (values - high.astype(jnp.float32)).astype(jnp.bfloat16)


def np_halves(values):
    values = values.astype(np.float32)
    high = values.astype(jnp.bfloat16)
    return high, (values - high.astype(np.float32)).astype(jnp.bfloat16)


def real_modes(positions, length, waves, is_sine):
    if isinstance(positions, int):
        positions = np.arange(positions)
    phase = (positions[:, None] * waves[None, :]) % length * (2.0 * np.pi / length)
    return np.where(is_sine[None, :], np.sin(phase), np.cos(phase))


def inverse_kernel(field_ref, modes_ref, back_ref, x_ref, out_ref):
    count, row_count, ny = field_ref.shape
    kbox = x_ref.shape[1] // 3
    owned = modes_ref.shape[2] // count
    parts = []
    for k in range(count):
        high, low = halves(modes_ref[0, :, k * owned : (k + 1) * owned].reshape(kbox, kbox))
        parts.append(
            lax.dot_general(
                x_ref[...],
                jnp.concatenate([high, low, high], 1),
                (((1,), (1,)), ((), ())),
                preferred_element_type=jnp.float32,
            )
        )
    high, low = halves(jnp.concatenate(parts, 0))
    added = jnp.dot(
        jnp.concatenate([high, low, high], 1), back_ref[...], preferred_element_type=jnp.float32
    )
    out_ref[...] = field_ref[...] + added.reshape(field_ref.shape)


def radices(devices):
    bits = devices.bit_length() - 1
    sizes = [2] * min(bits, 1)
    left = bits - len(sizes)
    return sizes + [2] * (left % 2) + [4] * (left // 2)


def stage_lags(sizes):
    steps = [LAGS[0]] + [LAGS[1] if size == 2 else LAGS[2] for size in sizes[1:]]
    steps = steps + steps[::-1]
    return [sum(steps[: stage + 1]) for stage in range(len(steps))]


def box_kernel(
    sizes, lags, norm, weights_hbm, cut_x_hbm, cut_y_hbm, index_hbm, field_hbm, table_hbm, base_hbm,
    turn_hbm, host_hbm, mix_hbm, back_hbm, full_ref, edge_ref, kept_field_ref, back_ref, x_ref,
    part_ref, want_ref, scale_ref, three_ref, table_ref, base_ref, turn_ref, host_ref, mix_ref,
    weights_ref, cut_x_ref, cut_y_ref, index_ref, *scratch
):
    phases = len(sizes)
    got, kept = scratch[:phases], scratch[phases : 2 * phases - 1]
    send_sem, recv_sem, load_sem, fetch_sem = scratch[2 * phases - 1 :]
    fields, row_count, ny = kept_field_ref.shape
    chunks, span, kbox = scale_ref.shape
    group = fields // chunks
    owned, khalf, levels = span // group, kbox // 2, cut_x_ref.shape[0]
    variables = fields // levels
    half = owned // 2
    me = lax.axis_index("row")
    member = lax.axis_index("member")
    strides = [1]
    for size in sizes:
        strides.append(strides[-1] * size)
    mine = [(me // strides[s]) % sizes[s] for s in range(phases)]
    barrier = pltpu.get_barrier_semaphore()

    def digit(step, away):
        return (mine[step] + away) % sizes[step]

    def peer(step, away):
        return (member, me + (digit(step, away) - mine[step]) * strides[step])

    def others(step):
        return range(1, sizes[step])

    def load(chunk):
        block = pl.ds(chunk * group, group)
        return pltpu.make_async_copy(
            field_hbm.at[block], kept_field_ref.at[block], load_sem.at[chunk]
        )

    early = [(table_hbm, table_ref), (base_hbm, base_ref), (turn_hbm.at[me], turn_ref)]
    late = [
        (host_hbm, host_ref), (mix_hbm, mix_ref), (weights_hbm, weights_ref),
        (cut_x_hbm, cut_x_ref), (cut_y_hbm, cut_y_ref), (index_hbm, index_ref),
    ]
    last = [(back_hbm.at[:kbox], back_ref.at[:kbox]), (back_hbm, back_ref.at[kbox:])]
    fetches = [
        pltpu.make_async_copy(source, target, fetch_sem.at[place])
        for place, (source, target) in enumerate(early + late + last)
    ]
    early, late, last = fetches[:3], fetches[3:9], fetches[9:]

    load(0).start()
    for fetch in early:
        fetch.start()
    for chunk in range(1, min(2, chunks)):
        load(chunk).start()
    for fetch in late:
        fetch.start()
    for chunk in range(2, chunks):
        load(chunk).start()
    for fetch in last:
        fetch.start()
    for step in range(phases):
        for away in others(step):
            pl.semaphore_signal(barrier, inc=1, device_id=peer(step, away), device_id_type=MESH)

    def lead(step, value):
        return (slice(None),) * (phases - 1 - step) + (value,)

    def remote(source, target, stage, chunk, step, away):
        return pltpu.make_async_remote_copy(
            src_ref=source,
            dst_ref=target,
            send_sem=send_sem.at[chunk, stage, away - 1],
            recv_sem=recv_sem.at[chunk, stage, away - 1],
            device_id=peer(step, away),
            device_id_type=MESH,
        )

    def held(step):
        return part_ref if step == 0 else kept[step - 1]

    def reduce_copy(step, chunk, away):
        source = held(step).at[(chunk,) + lead(step, digit(step, away))]
        return remote(source, got[step].at[chunk, away - 1], step, chunk, step, away)

    def gather_copy(step, chunk, away):
        fixed = tuple(mine[s] for s in range(step, -1, -1))
        block = full_ref.at[(chunk,) + (slice(None),) * (phases - 1 - step) + fixed]
        return remote(block, block, 2 * phases - 1 - step, chunk, step, away)

    def mixed(values):
        total = 0.0
        for _ in range(3):
            piece = values.astype(jnp.bfloat16)
            values = values - piece.astype(jnp.float32)
            total = total + lax.dot_general(
                piece,
                mix_ref[...],
                (((1,), (1,)), ((), ())),
                preferred_element_type=jnp.float32,
            )
        return total

    def prepare():
        for fetch in late:
            fetch.wait()
        edge = cut_x_ref[0]
        for level in range(levels):
            edge = jnp.maximum(edge, jnp.maximum(cut_x_ref[level], cut_y_ref[level]))
        edge_ref[0] = edge
        cosine, sine = [], []
        for b in range(half):
            plus, minus = host_ref[2 * b], host_ref[2 * b + 1]
            if b == 0:
                minus = jnp.where(me == 0, 0.0, minus)
            cosine.append(plus[0] + minus[0])
            sine.append(-(plus[1] + minus[1]))
        for b in range(half):
            plus, minus = host_ref[2 * b], host_ref[2 * b + 1]
            if b == 0:
                minus = jnp.where(me == 0, 0.0, minus)
            cosine.append(minus[1] - plus[1])
            sine.append(minus[0] - plus[0])
        rows = owned * fields
        cosine = jnp.stack(cosine).reshape(rows, kbox)
        sine = jnp.stack(sine).reshape(rows, kbox)
        modes = mixed(jnp.concatenate([cosine, sine], 1))
        slot = lax.broadcasted_iota(jnp.int32, (owned, kbox), 0)
        wave = me * half + slot % half
        across = lax.broadcasted_iota(jnp.int32, (owned, kbox), 1) % khalf
        times = jnp.where(wave == 0, 1.0, 2.0) * jnp.where(across == 0, norm, 2.0 * norm)
        for field in range(fields):
            variable, level = divmod(field, levels)
            chunk, place = divmod(field, group)
            inside = (across <= cut_x_ref[level]) & (wave <= cut_y_ref[level])
            scale = jnp.where(inside, weights_ref[variable, index_ref[level]], 0.0)
            wanted = [
                modes[(s * levels + level) * variables + variable][None] for s in range(owned)
            ]
            block = pl.ds(place * owned, owned)
            want_ref[chunk, block] = scale * jnp.concatenate(wanted, 0)
            scale_ref[chunk, block] = scale * times

    def advance(stage, chunk):
        if stage < phases:
            total = held(stage)[(chunk,) + lead(stage, mine[stage])]
            for away in others(stage):
                reduce_copy(stage, chunk, away).wait()
                total = total + got[stage][chunk, away - 1]
            if stage + 1 < phases:
                kept[stage][chunk] = total
                for away in others(stage + 1):
                    reduce_copy(stage + 1, chunk, away).start()
            else:
                own = tuple(mine[s] for s in range(phases - 1, -1, -1))
                full_ref[(chunk,) + own] = want_ref[chunk] - scale_ref[chunk] * total
                for away in others(phases - 1):
                    gather_copy(phases - 1, chunk, away).start()
        else:
            step = 2 * phases - 1 - stage
            for away in others(step):
                gather_copy(step, chunk, away).wait()
            if step > 0:
                for away in others(step - 1):
                    gather_copy(step - 1, chunk, away).start()

    def transform(chunk):
        load(chunk).wait()
        block = kept_field_ref[pl.ds(chunk * group, group)].reshape(group * row_count, ny)
        high, low = halves(block)
        both = jnp.dot(high, table_ref[...], preferred_element_type=jnp.float32)
        rest = jnp.dot(low, table_ref[:, :kbox], preferred_element_type=jnp.float32)
        part = both[:, :kbox] + both[:, kbox:] + rest
        cube = tuple(reversed(sizes))
        for k in range(group):
            high, low = halves(part[k * row_count : (k + 1) * row_count])
            moded = lax.dot_general(
                jnp.concatenate([high, low, high], 0),
                three_ref[...],
                (((0,), (0,)), ((), ())),
                preferred_element_type=jnp.float32,
            )
            where = (chunk,) + (slice(None),) * phases + (slice(k * owned, (k + 1) * owned),)
            part_ref[where] = moded.reshape(cube + (owned, kbox))

    for fetch in early:
        fetch.wait()
    turns = turn_ref[...]
    local = base_ref[:row_count] * turns[:1] + base_ref[row_count:] * turns[1:]
    x_high, x_low = halves(local)
    three_ref[...] = jnp.concatenate([x_high, x_high, x_low], 0)
    x_ref[...] = jnp.concatenate([x_high, x_high, x_low], 1)

    def tick(now, _):
        @pl.when(now < chunks)
        def _():
            transform(now)

        @pl.when(now == 0)
        def _():
            pl.semaphore_wait(barrier, sum(size - 1 for size in sizes))

        @pl.when(now < chunks)
        def _():
            for away in others(0):
                reduce_copy(0, now, away).start()

        @pl.when(now == PREPARE)
        def _():
            prepare()

        for stage in range(2 * phases):
            chunk = now - lags[stage]

            @pl.when((chunk >= 0) & (chunk < chunks))
            def _(stage=stage, chunk=chunk):
                advance(stage, chunk)

        return 0

    lax.fori_loop(0, chunks + lags[-1], tick, 0)
    for fetch in last:
        fetch.wait()


def box_modes(devices, chunks, scalars, field, table, base, turn, host, mix, back):
    fields, row_count, ny = field.shape
    owned, kbox = host.shape[0], host.shape[-1]
    span = fields // chunks * owned
    sizes = radices(devices)
    phases = len(sizes)
    cube = tuple(reversed(sizes))
    lags = stage_lags(sizes)

    def buffer(*shape):
        return pltpu.VMEM(shape + (span, kbox), jnp.float32)

    def like(array):
        return pltpu.VMEM(array.shape, array.dtype)

    got = [buffer(chunks, sizes[s] - 1, *cube[: phases - 1 - s]) for s in range(phases)]
    kept = [buffer(chunks, *cube[: phases - 1 - s]) for s in range(phases - 1)]
    smem = pl.BlockSpec(memory_space=pltpu.SMEM)
    vmem = pl.BlockSpec(memory_space=pltpu.VMEM)
    anywhere = pl.BlockSpec(memory_space=pl.ANY)
    widest = max(sizes) - 1
    return pl.pallas_call(
        functools.partial(box_kernel, sizes, lags, 1.0 / (row_count * devices * ny)),
        out_shape=(
            buffer(chunks, *cube),
            jax.ShapeDtypeStruct((1,), jnp.int32),
            pltpu.VMEM(field.shape, jnp.float32),
            pltpu.VMEM((3 * kbox, ny), jnp.bfloat16),
            pltpu.VMEM((row_count, 3 * kbox), jnp.bfloat16),
        ),
        in_specs=[anywhere] * 11,
        out_specs=(vmem, smem, vmem, vmem, vmem),
        scratch_shapes=[buffer(chunks, *cube)]
        + [buffer(chunks)] * 2
        + [pltpu.VMEM((3 * row_count, kbox), jnp.bfloat16)]
        + [like(table), like(base), pltpu.VMEM(turn.shape[1:], turn.dtype), like(host), like(mix)]
        + [pltpu.SMEM(array.shape, array.dtype) for array in scalars]
        + got
        + kept
        + [
            pltpu.SemaphoreType.DMA((chunks, 2 * phases, widest)),
            pltpu.SemaphoreType.DMA((chunks, 2 * phases, widest)),
            pltpu.SemaphoreType.DMA((chunks,)),
            pltpu.SemaphoreType.DMA((11,)),
        ],
        compiler_params=pltpu.CompilerParams(
            collective_id=0, has_side_effects=True, vmem_limit_bytes=VMEM_BYTES
        ),
    )(*scalars, field, table, base, turn, host, mix, back)


def nudge(field, host, weights, cut_x, cut_y, table_index):
    variables, levels, row_count, ny = field.shape
    owned, kbox = host.shape[0], host.shape[-1]
    khalf, half = kbox // 2, owned // 2
    devices = lax.axis_size("row")
    nx = row_count * devices
    fields = variables * levels
    group = max(size for size in range(1, GROUP + 1) if fields % size == 0)
    chunks = fields // group

    column = np.arange(kbox)
    y_wave = column // owned * half + column % half
    y_sine = column % owned >= half
    y_high, y_low = np_halves(real_modes(ny, ny, y_wave, y_sine))
    table_y = jnp.asarray(np.concatenate([y_high, y_low], 1))
    table_back = jnp.asarray(np.concatenate([y_high.T, y_low.T], 0))
    x_wave, x_sine = column % khalf, column >= khalf
    start = np.arange(devices) * row_count
    base = np.concatenate(
        [real_modes(row_count, nx, x_wave, column < 0), real_modes(row_count, nx, x_wave, column >= 0)]
    )
    turn_cos = real_modes(start, nx, x_wave, column < 0)
    turn_sin = real_modes(start, nx, x_wave, column >= 0)
    turn = np.stack(
        [np.where(x_sine, turn_sin, turn_cos), np.where(x_sine, turn_cos, -turn_sin)], 1
    )
    base = jnp.asarray(base.astype(np.float32))
    turn = jnp.asarray(turn.astype(np.float32))
    wave = column - khalf
    inside = np.abs(wave) < khalf
    mc = ((column[:, None] == np.abs(wave)[None, :]) & inside).astype(np.float32)
    ms = ((column[:, None] == np.abs(wave)[None, :] + khalf) & inside) * np.sign(wave)
    ms = ms.astype(np.float32)

    span = group * owned
    modes, edge, kept_field, back, local = box_modes(
        devices,
        chunks,
        (weights.T, cut_x, cut_y, table_index),
        field.reshape(fields, row_count, ny),
        table_y,
        base,
        turn,
        host.transpose(0, 1, 3, 2, 4),
        jnp.asarray(np.concatenate([mc, ms], 1)).astype(jnp.bfloat16),
        table_back,
    )
    modes = modes.reshape(chunks, devices, span, kbox)

    def inverse(kept_field, modes, back, local):
        grid_block = pl.BlockSpec((group, row_count, ny), lambda g: (g, 0, 0))
        result = pl.pallas_call(
            inverse_kernel,
            grid=(chunks,),
            out_shape=jax.ShapeDtypeStruct(kept_field.shape, jnp.float32),
            in_specs=[
                grid_block,
                pl.BlockSpec((1, devices, span, kbox), lambda g: (g, 0, 0, 0)),
                pl.BlockSpec(back.shape, lambda g: (0, 0)),
                pl.BlockSpec(local.shape, lambda g: (0, 0)),
            ],
            out_specs=grid_block,
            compiler_params=pltpu.CompilerParams(vmem_limit_bytes=VMEM_BYTES),
        )(kept_field, modes, back, local)
        return result.reshape(field.shape)

    return lax.cond(
        edge[0] >= khalf,
        lambda *args: general(*args[:6]),
        lambda *args: inverse(*args[6:]),
        field, host, weights, cut_x, cut_y, table_index, kept_field, modes, back, local,
    )


def solution(mesh):
    return jax.shard_map(
        nudge,
        mesh=mesh,
        in_specs=(
            P("member", None, "row", None),
            P("row", None, "member", None, None),
            P(),
            P(),
            P(),
            P(),
        ),
        out_specs=P("member", None, "row", None),
        check_vma=False,
    )
```

time: 65.3 us -> 53 us (0.81)
  Pallas kernels: 62.5 us -> 52.2 us
  local copies, waits for them, and re-layouts: 1.82 us -> 0.02 us
    pallas_call x2, Pallas kernels: 62.5 us -> 52.2 us  [the longest x1 39.9 us: box_modes(): pl.pallas_call(functools.partial(box_kernel, sizes, lags, 1.0 / (row_coun...]
    unnamed x15 -> x10, local copies, waits for them, and re-layouts: 1.09 us -> 0.02 us
    transpose x1 -> x0, local copies, waits for them, and re-layouts: 0.73 us -> none  [nudge(): placed = host.reshape(half, 2, 2, fields, kbox).transpose(2, 3, 1, 0, 4)]
where the time goes in v1:
time: 53 us; the launch traced here: 52.8 us
  Pallas kernels  52.2 us (98%)
  between operations  0.62 us (1%)
    pallas_call x1, Pallas kernels, box_modes(): pl.pallas_call(functools.partial(box_kernel, sizes, lags, 1.0 / (row_coun...  39.9 us
    pallas_call x1, Pallas kernels, inverse(): pl.pallas_call(inverse_kernel, grid=(chunks,), out_shape=jax.ShapeDtypeSt...  12.3 us

profile of v1, /device:TPU:0, one launch (start us, length us, event | category | flops | bytes accessed | tf_op | source)
XLA Modules:
  0.0 52.8 jit_solution(16886776669963324023)
XLA Ops:
  0.0 0.0 copy-start.1
  0.0 0.0 copy-start
  0.0 0.0 copy-start.2
  0.0 0.0 copy-start.3
  0.0 0.0 copy-start.4
  0.0 39.9 %shard_map.111 = (f32[8,4,2,2,24,128]{5,4,3,2,1,0:T(8,128)S(1)}, s32[1]{0:T(128)}, f32[24,128,2048]{2,1,0:T(8,128)S(1)}, bf16[384,2048]{1,0:T(8,128)(2,1)S(1)}, bf16[128,384]{1,0:T(8,128)(2,1)S(1)}) custom-call(f32[4,8]{1,0:T(4,128)} %bitcast.91, s32[6]{0:T(128)} %cut_x_hbm.1, s32[6]{0:T(128)} %cut_y_hbm.1, s32[6]{0:T(128)} %index_hbm.1, ...), custom_call_target="tpu_custom_call" | custom-call | tf_op jit(solution)/shard_map/pallas_call | solution.py:372
  40.5 0.0 copy-done.1
  40.5 0.0 copy-done
  40.5 0.0 copy-done.2
  40.5 0.0 copy-done.3
  40.5 0.0 copy-done.4
  40.5 12.3 %conditional.1 = (f32[4,6,128,2048]{3,2,1,0:T(8,128)}) conditional(s32[]{:T(128)} %bitcast.23, (f32[8,4,2,2,24,128]{5,4,3,2,1,0:T(8,128)S(1)}, f32[24,128,2048]{2,1,0:T(8,128)S(1)}, bf16[384,2048]{1,0:T(8,128)(2,1)S(1)}, bf16[128,384]{1,0:T(8,128)(2,1)S(1)}) %tuple.15, (f32[4,6,128,2048]{3,2,1,0:T(8,128)}, f32[8,2,4,6,128]{4,2,3,1,0:T(4,128)S(1)}, ...), branch_computations={%region_0.0_spmd, %region_1.5_spmd} | conditional | flops 1817103232 | bytes 17667372 | solution.py:468
  40.5 12.3 %branch_0_fun.1 = f32[24,128,2048]{2,1,0:T(8,128)} custom-call(f32[24,128,2048]{2,1,0:T(8,128)S(1)} %get-tuple-element.57.field_ref, f32[8,16,24,128]{3,2,1,0:T(8,128)S(1)} %bitcast.82, bf16[384,2048]{1,0:T(8,128)(2,1)S(1)} %get-tuple-element.59.back_ref, bf16[128,384]{1,0:T(8,128)(2,1)S(1)} %get-tuple-element.60.x_ref), custom_call_target="tpu_custom_call" | custom-call | tf_op jit(solution)/shard_map/cond/branch_0_fun/pallas_call | solution.py:453
Async XLA Ops:
  0.0 40.5 %copy-start.1 = (f32[8,4]{0,1:T(4,128)S(1)}, f32[8,4]{0,1:T(4,128)}, u32[]{:S(2)}) copy-start(f32[8,4]{0,1:T(4,128)} %param.17) | copy-start | bytes 388
  0.0 40.5 %copy-start = (f32[8,2,4,6,128]{4,2,3,1,0:T(4,128)S(1)}, f32[8,2,4,6,128]{4,2,3,1,0:T(4,128)}, u32[]{:S(2)}) copy-start(f32[8,2,4,6,128]{4,2,3,1,0:T(4,128)} %param.16) | copy-start | bytes 589828
  0.0 40.5 %copy-start.2 = (s32[6]{0:T(128)S(1)}, s32[6]{0:T(128)}, u32[]{:S(2)}) copy-start(s32[6]{0:T(128)} %cut_x_hbm.1) | copy-start | bytes 76
  0.0 40.5 %copy-start.3 = (s32[6]{0:T(128)S(1)}, s32[6]{0:T(128)}, u32[]{:S(2)}) copy-start(s32[6]{0:T(128)} %cut_y_hbm.1) | copy-start | bytes 76
  0.0 40.5 %copy-start.4 = (s32[6]{0:T(128)S(1)}, s32[6]{0:T(128)}, u32[]{:S(2)}) copy-start(s32[6]{0:T(128)} %index_hbm.1) | copy-start | bytes 76

commit v2 on v1

--- a/solution.py
+++ b/solution.py
@@ -13,8 +13,9 @@
 MESH = pl.DeviceIdType.MESH
 VMEM_BYTES = 36_000_000
 GROUP = 3
-LAGS = (1, 2, 3)
+LAGS = (1, 2, 2)
 PREPARE = 1
+AHEAD = 3
 HIGHEST = lax.Precision.HIGHEST
 
 
@@ -88,13 +89,32 @@
     return np.where(is_sine[None, :], np.sin(phase), np.cos(phase))
 
 
-def inverse_kernel(field_ref, modes_ref, back_ref, x_ref, out_ref):
-    count, row_count, ny = field_ref.shape
+def inverse_kernel(field_ref, modes_ref, back_ref, x_ref, out_hbm, out_ref, sem):
+    chunks, count = field_ref.shape[:2]
+    owned = modes_ref.shape[2] // count
+
+    def store(chunk):
+        return pltpu.make_async_copy(out_ref.at[chunk], out_hbm.at[chunk], sem.at[chunk])
+
+    def step(chunk, _):
+        inverse_step(chunk, count, owned, field_ref, modes_ref, back_ref, x_ref, out_ref)
+        store(chunk).start()
+        return 0
+
+    lax.fori_loop(0, chunks, step, 0)
+    for chunk in range(chunks):
+        store(chunk).wait()
+
+
+def inverse_step(chunk, count, owned, field_ref, modes_ref, back_ref, x_ref, out_ref):
+    row_count, ny = field_ref.shape[2:]
     kbox = x_ref.shape[1] // 3
-    owned = modes_ref.shape[2] // count
     parts = []
     for k in range(count):
-        high, low = halves(modes_ref[0, :, k * owned : (k + 1) * owned].reshape(kbox, kbox))
+        block = modes_ref[chunk, :, k * owned : (k + 1) * owned]
+        swapped = jnp.concatenate([block[:, owned // 2 :], block[:, : owned // 2]], 1)
+        both = jnp.concatenate([block.reshape(kbox, kbox), swapped.reshape(kbox, kbox)], 0)
+        high, low = halves(both)
         parts.append(
             lax.dot_general(
                 x_ref[...],
@@ -103,11 +123,24 @@
                 preferred_element_type=jnp.float32,
             )
         )
-    high, low = halves(jnp.concatenate(parts, 0))
-    added = jnp.dot(
-        jnp.concatenate([high, low, high], 1), back_ref[...], preferred_element_type=jnp.float32
-    )
-    out_ref[...] = field_ref[...] + added.reshape(field_ref.shape)
+    spread = jnp.concatenate(parts, 0)
+    high = spread[:, :kbox].astype(jnp.bfloat16)
+    low = (spread[:, kbox:] - spread[:, kbox:].astype(jnp.bfloat16).astype(jnp.float32)).astype(
+        jnp.bfloat16
+    )
+    lane = lax.broadcasted_iota(jnp.int32, high.shape, 1)
+    first = lane % owned < owned // 2
+    even = jnp.where(first, high, low)
+    odd = jnp.where(first, low, high)
+    shape = (count, row_count, ny // 2)
+    plus = jnp.dot(
+        jnp.concatenate([even, even], 1), back_ref[0], preferred_element_type=jnp.float32
+    ).reshape(shape)
+    minus = jnp.dot(
+        jnp.concatenate([odd, odd], 1), back_ref[1], preferred_element_type=jnp.float32
+    ).reshape(shape)
+    out_ref[chunk, :, :, : ny // 2] = field_ref[chunk, :, :, : ny // 2] + (plus + minus)
+    out_ref[chunk, :, :, ny // 2 :] = field_ref[chunk, :, :, ny // 2 :] + (plus - minus)
 
 
 def radices(devices):
@@ -166,7 +199,7 @@
         (host_hbm, host_ref), (mix_hbm, mix_ref), (weights_hbm, weights_ref),
         (cut_x_hbm, cut_x_ref), (cut_y_hbm, cut_y_ref), (index_hbm, index_ref),
     ]
-    last = [(back_hbm.at[:kbox], back_ref.at[:kbox]), (back_hbm, back_ref.at[kbox:])]
+    last = [(back_hbm, back_ref)]
     fetches = [
         pltpu.make_async_copy(source, target, fetch_sem.at[place])
         for place, (source, target) in enumerate(early + late + last)
@@ -176,14 +209,10 @@
     load(0).start()
     for fetch in early:
         fetch.start()
-    for chunk in range(1, min(2, chunks)):
-        load(chunk).start()
     for fetch in late:
         fetch.start()
-    for chunk in range(2, chunks):
+    for chunk in range(1, min(AHEAD, chunks)):
         load(chunk).start()
-    for fetch in last:
-        fetch.start()
     for step in range(phases):
         for away in others(step):
             pl.semaphore_signal(barrier, inc=1, device_id=peer(step, away), device_id_type=MESH)
@@ -234,24 +263,23 @@
             edge = jnp.maximum(edge, jnp.maximum(cut_x_ref[level], cut_y_ref[level]))
         edge_ref[0] = edge
         cosine, sine = [], []
-        for b in range(half):
-            plus, minus = host_ref[2 * b], host_ref[2 * b + 1]
-            if b == 0:
+        for place in range(owned):
+            pair = 2 * (place % (half // 2)) + place // half
+            plus, minus = host_ref[2 * pair], host_ref[2 * pair + 1]
+            if pair == 0:
                 minus = jnp.where(me == 0, 0.0, minus)
-            cosine.append(plus[0] + minus[0])
-            sine.append(-(plus[1] + minus[1]))
-        for b in range(half):
-            plus, minus = host_ref[2 * b], host_ref[2 * b + 1]
-            if b == 0:
-                minus = jnp.where(me == 0, 0.0, minus)
-            cosine.append(minus[1] - plus[1])
-            sine.append(minus[0] - plus[0])
+            if place // (half // 2) % 2 == 0:
+                cosine.append(plus[0] + minus[0])
+                sine.append(-(plus[1] + minus[1]))
+            else:
+                cosine.append(minus[1] - plus[1])
+                sine.append(minus[0] - plus[0])
         rows = owned * fields
         cosine = jnp.stack(cosine).reshape(rows, kbox)
         sine = jnp.stack(sine).reshape(rows, kbox)
         modes = mixed(jnp.concatenate([cosine, sine], 1))
         slot = lax.broadcasted_iota(jnp.int32, (owned, kbox), 0)
-        wave = me * half + slot % half
+        wave = me * half + 2 * (slot % (half // 2)) + slot // half
         across = lax.broadcasted_iota(jnp.int32, (owned, kbox), 1) % khalf
         times = jnp.where(wave == 0, 1.0, 2.0) * jnp.where(across == 0, norm, 2.0 * norm)
         for field in range(fields):
@@ -291,6 +319,11 @@
 
     def transform(chunk):
         load(chunk).wait()
+
+        @pl.when(chunk + AHEAD < chunks)
+        def _():
+            load(chunk + AHEAD).start()
+
         block = kept_field_ref[pl.ds(chunk * group, group)].reshape(group * row_count, ny)
         high, low = halves(block)
         both = jnp.dot(high, table_ref[...], preferred_element_type=jnp.float32)
@@ -334,6 +367,11 @@
         def _():
             prepare()
 
+        @pl.when(now == chunks - 1)
+        def _():
+            for fetch in last:
+                fetch.start()
+
         for stage in range(2 * phases):
             chunk = now - lags[stage]
 
@@ -375,7 +413,7 @@
             buffer(chunks, *cube),
             jax.ShapeDtypeStruct((1,), jnp.int32),
             pltpu.VMEM(field.shape, jnp.float32),
-            pltpu.VMEM((3 * kbox, ny), jnp.bfloat16),
+            like(back),
             pltpu.VMEM((row_count, 3 * kbox), jnp.bfloat16),
         ),
         in_specs=[anywhere] * 11,
@@ -391,7 +429,7 @@
             pltpu.SemaphoreType.DMA((chunks, 2 * phases, widest)),
             pltpu.SemaphoreType.DMA((chunks, 2 * phases, widest)),
             pltpu.SemaphoreType.DMA((chunks,)),
-            pltpu.SemaphoreType.DMA((11,)),
+            pltpu.SemaphoreType.DMA((10,)),
         ],
         compiler_params=pltpu.CompilerParams(
             collective_id=0, has_side_effects=True, vmem_limit_bytes=VMEM_BYTES
@@ -410,11 +448,16 @@
     chunks = fields // group
 
     column = np.arange(kbox)
-    y_wave = column // owned * half + column % half
-    y_sine = column % owned >= half
+    y_odd, y_sine, y_place = column // half % 2, column // (half // 2) % 2 == 1, column % (half // 2)
+    y_wave = column // owned * half + 2 * y_place + y_odd
     y_high, y_low = np_halves(real_modes(ny, ny, y_wave, y_sine))
     table_y = jnp.asarray(np.concatenate([y_high, y_low], 1))
-    table_back = jnp.asarray(np.concatenate([y_high.T, y_low.T], 0))
+    backs = []
+    for odd in (0, 1):
+        twin = np.where(y_odd == odd, column, (column + half) % owned + column // owned * owned)
+        high, low = np_halves(real_modes(ny // 2, ny, y_wave[twin], y_sine[twin]).T)
+        backs.append(np.concatenate([high, low], 0))
+    table_back = jnp.asarray(np.stack(backs))
     x_wave, x_sine = column % khalf, column >= khalf
     start = np.arange(devices) * row_count
     base = np.concatenate(
@@ -449,20 +492,18 @@
     modes = modes.reshape(chunks, devices, span, kbox)
 
     def inverse(kept_field, modes, back, local):
-        grid_block = pl.BlockSpec((group, row_count, ny), lambda g: (g, 0, 0))
+        split = (chunks, group, row_count, ny)
+        vmem = pl.BlockSpec(memory_space=pltpu.VMEM)
         result = pl.pallas_call(
             inverse_kernel,
-            grid=(chunks,),
-            out_shape=jax.ShapeDtypeStruct(kept_field.shape, jnp.float32),
-            in_specs=[
-                grid_block,
-                pl.BlockSpec((1, devices, span, kbox), lambda g: (g, 0, 0, 0)),
-                pl.BlockSpec(back.shape, lambda g: (0, 0)),
-                pl.BlockSpec(local.shape, lambda g: (0, 0)),
+            out_shape=jax.ShapeDtypeStruct(split, jnp.float32),
+            in_specs=[vmem] * 4,
+            out_specs=pl.BlockSpec(memory_space=pl.ANY),
+            scratch_shapes=[
+                pltpu.VMEM(split, jnp.float32), pltpu.SemaphoreType.DMA((chunks,))
             ],
-            out_specs=grid_block,
             compiler_params=pltpu.CompilerParams(vmem_limit_bytes=VMEM_BYTES),
-        )(kept_field, modes, back, local)
+        )(kept_field.reshape(split), modes, back, local)
         return result.reshape(field.shape)
 
     return lax.cond(

time: 53 us -> 50.2 us (0.947)
  Pallas kernels: 52.2 us -> 49.1 us
    pallas_call x1, Pallas kernels: 12.3 us -> 9.49 us  [inverse(): pl.pallas_call(inverse_kernel, out_shape=jax.ShapeDtypeStruct(split, jnp....]
where the time goes in v2:
time: 50.2 us; the launch traced here: 50.1 us
  Pallas kernels  49.1 us (98%)
  between operations  0.78 us (2%)
    pallas_call x1, Pallas kernels, box_modes(): pl.pallas_call(functools.partial(box_kernel, sizes, lags, 1.0 / (row_coun...  39.6 us
    pallas_call x1, Pallas kernels, inverse(): pl.pallas_call(inverse_kernel, out_shape=jax.ShapeDtypeStruct(split, jnp....  9.49 us

profile of v2, /device:TPU:0, one launch (start us, length us, event | category | flops | bytes accessed | tf_op | source)
XLA Modules:
  0.0 50.1 jit_solution(12744675292587773163)
XLA Ops:
  0.0 0.0 copy-start.1
  0.0 0.0 copy-start
  0.0 0.0 copy-start.2
  0.0 0.0 copy-start.3
  0.0 0.0 copy-start.4
  0.0 39.6 %shard_map.111 = (f32[8,4,2,2,24,128]{5,4,3,2,1,0:T(8,128)S(1)}, s32[1]{0:T(128)}, f32[24,128,2048]{2,1,0:T(8,128)S(1)}, bf16[2,256,1024]{2,1,0:T(8,128)(2,1)S(1)}, bf16[128,384]{1,0:T(8,128)(2,1)S(1)}) custom-call(f32[4,8]{1,0:T(4,128)} %bitcast.93, s32[6]{0:T(128)} %cut_x_hbm.1, s32[6]{0:T(128)} %cut_y_hbm.1, s32[6]{0:T(128)} %index_hbm.1, ...), custom_call_target="tpu_custom_call" | custom-call | tf_op jit(solution)/shard_map/pallas_call | solution.py:410
  40.2 0.0 copy-done.1
  40.2 0.0 copy-done
  40.2 0.0 copy-done.2
  40.2 0.0 copy-done.3
  40.2 0.0 copy-done.4
  40.2 9.7 %conditional.1 = (f32[4,6,128,2048]{3,2,1,0:T(8,128)}) conditional(s32[]{:T(128)} %bitcast.24, (f32[24,128,2048]{2,1,0:T(8,128)S(1)}, f32[8,4,2,2,24,128]{5,4,3,2,1,0:T(8,128)S(1)}, bf16[2,256,1024]{2,1,0:T(8,128)(2,1)S(1)}, bf16[128,384]{1,0:T(8,128)(2,1)S(1)}) %tuple.15, (f32[4,6,128,2048]{3,2,1,0:T(8,128)}, f32[8,2,4,6,128]{4,2,3,1,0:T(4,128)S(1)}, ...), branch_computations={%region_0.0_spmd, %region_1.5_spmd} | conditional | flops 1817103232 | bytes 17667372 | solution.py:509
  40.2 9.5 %branch_0_fun.1 = f32[8,3,128,2048]{3,2,1,0:T(8,128)} custom-call(f32[8,3,128,2048]{3,2,1,0:T(8,128)S(1)} %bitcast.83, f32[8,16,24,128]{3,2,1,0:T(8,128)S(1)} %bitcast.84, bf16[2,256,1024]{2,1,0:T(8,128)(2,1)S(1)} %get-tuple-element.59.back_ref, bf16[128,384]{1,0:T(8,128)(2,1)S(1)} %get-tuple-element.60.x_ref), custom_call_target="tpu_custom_call" | custom-call | tf_op jit(solution)/shard_map/cond/branch_0_fun/pallas_call | solution.py:497
Async XLA Ops:
  0.0 40.2 %copy-start.1 = (f32[8,4]{0,1:T(4,128)S(1)}, f32[8,4]{0,1:T(4,128)}, u32[]{:S(2)}) copy-start(f32[8,4]{0,1:T(4,128)} %param.17) | copy-start | bytes 388
  0.0 40.2 %copy-start = (f32[8,2,4,6,128]{4,2,3,1,0:T(4,128)S(1)}, f32[8,2,4,6,128]{4,2,3,1,0:T(4,128)}, u32[]{:S(2)}) copy-start(f32[8,2,4,6,128]{4,2,3,1,0:T(4,128)} %param.16) | copy-start | bytes 589828
  0.0 40.2 %copy-start.2 = (s32[6]{0:T(128)S(1)}, s32[6]{0:T(128)}, u32[]{:S(2)}) copy-start(s32[6]{0:T(128)} %cut_x_hbm.1) | copy-start | bytes 76
  0.0 40.2 %copy-start.3 = (s32[6]{0:T(128)S(1)}, s32[6]{0:T(128)}, u32[]{:S(2)}) copy-start(s32[6]{0:T(128)} %cut_y_hbm.1) | copy-start | bytes 76
  0.0 40.2 %copy-start.4 = (s32[6]{0:T(128)S(1)}, s32[6]{0:T(128)}, u32[]{:S(2)}) copy-start(s32[6]{0:T(128)} %index_hbm.1) | copy-start | bytes 76

commit v3 on v2

--- a/solution.py
+++ b/solution.py
@@ -15,6 +15,7 @@
 GROUP = 3
 LAGS = (1, 2, 2)
 PREPARE = 1
+READY = 1
 AHEAD = 3
 HIGHEST = lax.Precision.HIGHEST
 
@@ -91,27 +92,29 @@
 
 def inverse_kernel(field_ref, modes_ref, back_ref, x_ref, out_hbm, out_ref, sem):
     chunks, count = field_ref.shape[:2]
-    owned = modes_ref.shape[2] // count
-
-    def store(chunk):
-        return pltpu.make_async_copy(out_ref.at[chunk], out_hbm.at[chunk], sem.at[chunk])
+
+    def store(chunk, source):
+        return pltpu.make_async_copy(source.at[chunk], out_hbm.at[chunk], sem.at[chunk])
 
     def step(chunk, _):
-        inverse_step(chunk, count, owned, field_ref, modes_ref, back_ref, x_ref, out_ref)
-        store(chunk).start()
+        inverse_step(count, field_ref.at[chunk], modes_ref[chunk], back_ref, x_ref, out_ref.at[chunk])
+        store(chunk, out_ref).start()
         return 0
 
-    lax.fori_loop(0, chunks, step, 0)
+    for chunk in range(READY):
+        store(chunk, field_ref).start()
+    lax.fori_loop(READY, chunks, step, 0)
     for chunk in range(chunks):
-        store(chunk).wait()
-
-
-def inverse_step(chunk, count, owned, field_ref, modes_ref, back_ref, x_ref, out_ref):
-    row_count, ny = field_ref.shape[2:]
+        store(chunk, field_ref if chunk < READY else out_ref).wait()
+
+
+def inverse_step(count, field_ref, modes, back_ref, x_ref, out_ref):
+    row_count, ny = field_ref.shape[1:]
     kbox = x_ref.shape[1] // 3
+    owned = modes.shape[1] // count
     parts = []
     for k in range(count):
-        block = modes_ref[chunk, :, k * owned : (k + 1) * owned]
+        block = modes[:, k * owned : (k + 1) * owned]
         swapped = jnp.concatenate([block[:, owned // 2 :], block[:, : owned // 2]], 1)
         both = jnp.concatenate([block.reshape(kbox, kbox), swapped.reshape(kbox, kbox)], 0)
         high, low = halves(both)
@@ -139,8 +142,8 @@
     minus = jnp.dot(
         jnp.concatenate([odd, odd], 1), back_ref[1], preferred_element_type=jnp.float32
     ).reshape(shape)
-    out_ref[chunk, :, :, : ny // 2] = field_ref[chunk, :, :, : ny // 2] + (plus + minus)
-    out_ref[chunk, :, :, ny // 2 :] = field_ref[chunk, :, :, ny // 2 :] + (plus - minus)
+    out_ref[:, :, : ny // 2] = field_ref[:, :, : ny // 2] + (plus + minus)
+    out_ref[:, :, ny // 2 :] = field_ref[:, :, ny // 2 :] + (plus - minus)
 
 
 def radices(devices):
@@ -379,11 +382,20 @@
             def _(stage=stage, chunk=chunk):
                 advance(stage, chunk)
 
+        for chunk in range(READY):
+
+            @pl.when(now == lags[-1] + 1 + chunk)
+            def _(chunk=chunk):
+                if chunk == 0:
+                    for fetch in last:
+                        fetch.wait()
+                block = kept_field_ref.at[pl.ds(chunk * group, group)]
+                modes = full_ref[chunk].reshape(math.prod(sizes), span, kbox)
+                inverse_step(group, block, modes, back_ref, x_ref, block)
+
         return 0
 
     lax.fori_loop(0, chunks + lags[-1], tick, 0)
-    for fetch in last:
-        fetch.wait()
 
 
 def box_modes(devices, chunks, scalars, field, table, base, turn, host, mix, back):

time: 50.2 us -> 49.8 us (level)
    pallas_call x1, Pallas kernels: 9.49 us -> 8.54 us  [inverse(): pl.pallas_call(inverse_kernel, out_shape=jax.ShapeDtypeStruct(split, jnp....]
    pallas_call x1, Pallas kernels: 39.6 us -> 40.1 us  [box_modes(): pl.pallas_call(functools.partial(box_kernel, sizes, lags, 1.0 / (row_coun...]
where the time goes in v3:
time: 49.8 us; the launch traced here: 49.6 us
  Pallas kernels  48.6 us (98%)
  between operations  0.78 us (2%)
    pallas_call x1, Pallas kernels, box_modes(): pl.pallas_call(functools.partial(box_kernel, sizes, lags, 1.0 / (row_coun...  40.1 us
    pallas_call x1, Pallas kernels, inverse(): pl.pallas_call(inverse_kernel, out_shape=jax.ShapeDtypeStruct(split, jnp....  8.54 us

profile of v3, /device:TPU:0, one launch (start us, length us, event | category | flops | bytes accessed | tf_op | source)
XLA Modules:
  0.0 49.6 jit_solution(5190435582602580685)
XLA Ops:
  0.0 0.0 copy-start.1
  0.0 0.0 copy-start
  0.0 0.0 copy-start.2
  0.0 0.0 copy-start.3
  0.0 0.0 copy-start.4
  0.0 40.1 %shard_map.111 = (f32[8,4,2,2,24,128]{5,4,3,2,1,0:T(8,128)S(1)}, s32[1]{0:T(128)}, f32[24,128,2048]{2,1,0:T(8,128)S(1)}, bf16[2,256,1024]{2,1,0:T(8,128)(2,1)S(1)}, bf16[128,384]{1,0:T(8,128)(2,1)S(1)}) custom-call(f32[4,8]{1,0:T(4,128)} %bitcast.93, s32[6]{0:T(128)} %cut_x_hbm.1, s32[6]{0:T(128)} %cut_y_hbm.1, s32[6]{0:T(128)} %index_hbm.1, ...), custom_call_target="tpu_custom_call" | custom-call | tf_op jit(solution)/shard_map/pallas_call | solution.py:422
  40.7 0.0 copy-done.1
  40.7 0.0 copy-done
  40.7 0.0 copy-done.2
  40.7 0.0 copy-done.3
  40.7 0.0 copy-done.4
  40.7 8.7 %conditional.1 = (f32[4,6,128,2048]{3,2,1,0:T(8,128)}) conditional(s32[]{:T(128)} %bitcast.24, (f32[24,128,2048]{2,1,0:T(8,128)S(1)}, f32[8,4,2,2,24,128]{5,4,3,2,1,0:T(8,128)S(1)}, bf16[2,256,1024]{2,1,0:T(8,128)(2,1)S(1)}, bf16[128,384]{1,0:T(8,128)(2,1)S(1)}) %tuple.15, (f32[4,6,128,2048]{3,2,1,0:T(8,128)}, f32[8,2,4,6,128]{4,2,3,1,0:T(4,128)S(1)}, ...), branch_computations={%region_0.0_spmd, %region_1.5_spmd} | conditional | flops 1817103232 | bytes 17667372 | solution.py:521
  40.7 8.5 %branch_0_fun.1 = f32[8,3,128,2048]{3,2,1,0:T(8,128)} custom-call(f32[8,3,128,2048]{3,2,1,0:T(8,128)S(1)} %bitcast.83, f32[8,16,24,128]{3,2,1,0:T(8,128)S(1)} %bitcast.84, bf16[2,256,1024]{2,1,0:T(8,128)(2,1)S(1)} %get-tuple-element.59.back_ref, bf16[128,384]{1,0:T(8,128)(2,1)S(1)} %get-tuple-element.60.x_ref), custom_call_target="tpu_custom_call" | custom-call | tf_op jit(solution)/shard_map/cond/branch_0_fun/pallas_call | solution.py:509
Async XLA Ops:
  0.0 40.7 %copy-start.1 = (f32[8,4]{0,1:T(4,128)S(1)}, f32[8,4]{0,1:T(4,128)}, u32[]{:S(2)}) copy-start(f32[8,4]{0,1:T(4,128)} %param.17) | copy-start | bytes 388
  0.0 40.7 %copy-start = (f32[8,2,4,6,128]{4,2,3,1,0:T(4,128)S(1)}, f32[8,2,4,6,128]{4,2,3,1,0:T(4,128)}, u32[]{:S(2)}) copy-start(f32[8,2,4,6,128]{4,2,3,1,0:T(4,128)} %param.16) | copy-start | bytes 589828
  0.0 40.7 %copy-start.2 = (s32[6]{0:T(128)S(1)}, s32[6]{0:T(128)}, u32[]{:S(2)}) copy-start(s32[6]{0:T(128)} %cut_x_hbm.1) | copy-start | bytes 76
  0.0 40.7 %copy-start.3 = (s32[6]{0:T(128)S(1)}, s32[6]{0:T(128)}, u32[]{:S(2)}) copy-start(s32[6]{0:T(128)} %cut_y_hbm.1) | copy-start | bytes 76
  0.0 40.7 %copy-start.4 = (s32[6]{0:T(128)S(1)}, s32[6]{0:T(128)}, u32[]{:S(2)}) copy-start(s32[6]{0:T(128)} %index_hbm.1) | copy-start | bytes 76

commit v4 on v3

--- a/solution.py
+++ b/solution.py
@@ -14,7 +14,7 @@
 VMEM_BYTES = 36_000_000
 GROUP = 3
 LAGS = (1, 2, 2)
-PREPARE = 1
+PREPARE = 3
 READY = 1
 AHEAD = 3
 HIGHEST = lax.Precision.HIGHEST
@@ -155,7 +155,8 @@
 
 def stage_lags(sizes):
     steps = [LAGS[0]] + [LAGS[1] if size == 2 else LAGS[2] for size in sizes[1:]]
-    steps = steps + steps[::-1]
+    up = [step + (size == 2 and s > 0) for s, (step, size) in enumerate(zip(steps, sizes))]
+    steps = steps + up[::-1]
     return [sum(steps[: stage + 1]) for stage in range(len(steps))]
 
 

time: 49.8 us -> 49.3 us (0.990)
  Pallas kernels: 48.6 us -> 48.1 us
    pallas_call x1, Pallas kernels: 40.1 us -> 39.6 us  [box_modes(): pl.pallas_call(functools.partial(box_kernel, sizes, lags, 1.0 / (row_coun...]
where the time goes in v4:
time: 49.3 us; the launch traced here: 49.1 us
  Pallas kernels  48.1 us (98%)
  between operations  0.78 us (2%)
    pallas_call x1, Pallas kernels, box_modes(): pl.pallas_call(functools.partial(box_kernel, sizes, lags, 1.0 / (row_coun...  39.6 us
    pallas_call x1, Pallas kernels, inverse(): pl.pallas_call(inverse_kernel, out_shape=jax.ShapeDtypeStruct(split, jnp....  8.54 us

profile of v4, /device:TPU:0, one launch (start us, length us, event | category | flops | bytes accessed | tf_op | source)
XLA Modules:
  0.0 49.1 jit_solution(3727464600063553735)
XLA Ops:
  0.0 0.0 copy-start.1
  0.0 0.0 copy-start
  0.0 0.0 copy-start.2
  0.0 0.0 copy-start.3
  0.0 0.0 copy-start.4
  0.0 39.6 %shard_map.111 = (f32[8,4,2,2,24,128]{5,4,3,2,1,0:T(8,128)S(1)}, s32[1]{0:T(128)}, f32[24,128,2048]{2,1,0:T(8,128)S(1)}, bf16[2,256,1024]{2,1,0:T(8,128)(2,1)S(1)}, bf16[128,384]{1,0:T(8,128)(2,1)S(1)}) custom-call(f32[4,8]{1,0:T(4,128)} %bitcast.93, s32[6]{0:T(128)} %cut_x_hbm.1, s32[6]{0:T(128)} %cut_y_hbm.1, s32[6]{0:T(128)} %index_hbm.1, ...), custom_call_target="tpu_custom_call" | custom-call | tf_op jit(solution)/shard_map/pallas_call | solution.py:423
  40.2 0.0 copy-done.1
  40.2 0.0 copy-done
  40.2 0.0 copy-done.2
  40.2 0.0 copy-done.3
  40.2 0.0 copy-done.4
  40.2 8.7 %conditional.1 = (f32[4,6,128,2048]{3,2,1,0:T(8,128)}) conditional(s32[]{:T(128)} %bitcast.24, (f32[24,128,2048]{2,1,0:T(8,128)S(1)}, f32[8,4,2,2,24,128]{5,4,3,2,1,0:T(8,128)S(1)}, bf16[2,256,1024]{2,1,0:T(8,128)(2,1)S(1)}, bf16[128,384]{1,0:T(8,128)(2,1)S(1)}) %tuple.15, (f32[4,6,128,2048]{3,2,1,0:T(8,128)}, f32[8,2,4,6,128]{4,2,3,1,0:T(4,128)S(1)}, ...), branch_computations={%region_0.0_spmd, %region_1.5_spmd} | conditional | flops 1817103232 | bytes 17667372 | solution.py:522
  40.2 8.5 %branch_0_fun.1 = f32[8,3,128,2048]{3,2,1,0:T(8,128)} custom-call(f32[8,3,128,2048]{3,2,1,0:T(8,128)S(1)} %bitcast.83, f32[8,16,24,128]{3,2,1,0:T(8,128)S(1)} %bitcast.84, bf16[2,256,1024]{2,1,0:T(8,128)(2,1)S(1)} %get-tuple-element.59.back_ref, bf16[128,384]{1,0:T(8,128)(2,1)S(1)} %get-tuple-element.60.x_ref), custom_call_target="tpu_custom_call" | custom-call | tf_op jit(solution)/shard_map/cond/branch_0_fun/pallas_call | solution.py:510
Async XLA Ops:
  0.0 40.2 %copy-start.1 = (f32[8,4]{0,1:T(4,128)S(1)}, f32[8,4]{0,1:T(4,128)}, u32[]{:S(2)}) copy-start(f32[8,4]{0,1:T(4,128)} %param.17) | copy-start | bytes 388
  0.0 40.2 %copy-start = (f32[8,2,4,6,128]{4,2,3,1,0:T(4,128)S(1)}, f32[8,2,4,6,128]{4,2,3,1,0:T(4,128)}, u32[]{:S(2)}) copy-start(f32[8,2,4,6,128]{4,2,3,1,0:T(4,128)} %param.16) | copy-start | bytes 589828
  0.0 40.2 %copy-start.2 = (s32[6]{0:T(128)S(1)}, s32[6]{0:T(128)}, u32[]{:S(2)}) copy-start(s32[6]{0:T(128)} %cut_x_hbm.1) | copy-start | bytes 76
  0.0 40.2 %copy-start.3 = (s32[6]{0:T(128)S(1)}, s32[6]{0:T(128)}, u32[]{:S(2)}) copy-start(s32[6]{0:T(128)} %cut_y_hbm.1) | copy-start | bytes 76
  0.0 40.2 %copy-start.4 = (s32[6]{0:T(128)S(1)}, s32[6]{0:T(128)}, u32[]{:S(2)}) copy-start(s32[6]{0:T(128)} %index_hbm.1) | copy-start | bytes 76
